TPU v7x, 32 devices: a whole 2x2x4 slice. The times are simulated.
32 devices in a mesh: gx: 4 (over x, core), gy: 4 (over z), gz: 2 (over y).
Axes of the slice: x: 2, y: 2, z: 4, core: 2. Of those that a mesh axis runs over, the one named last changes fastest.
Arguments:
- fields: float32 [11, 500, 32, 256], P(None, 'gx', 'gy', 'gz'), may hold values from -6 to 6
- var_scale: float32 [11], replicated, may hold values from 0.3 to 3
- start_basis: float32 [500, 64], replicated, may hold values from -6 to 6
Outputs:
- factor: float32 [500, 64], replicated
- core: float32 [64, 11, 32, 256], P('gx', None, 'gy', 'gz')
All inputs are finite; a program needn't handle non-finite values.
Results may differ from a plain program's by a relative error of at most 0.0002.
Values sent between devices are 32-bit elements; how exact they have to be, the bound alone decides.
A program may use at most 128 MiB of HBM per device.

v0:
```python
import jax
import jax.numpy as jnp
from jax import lax
from jax.sharding import PartitionSpec as P

ITERS = 3


def orthonormal(block):
    small = jnp.dot(block.T, block, precision=lax.Precision.HIGHEST)
    lower = jnp.linalg.cholesky(small)
    return jax.scipy.linalg.solve_triangular(lower, block.T, lower=True).T


def per_device(fields, var_scale, start_basis):
    scaled = fields * var_scale[:, None, None, None]
    rows_dev = scaled.shape[1]
    contract = (((0, 2, 3), (0, 2, 3)), ((), ()))
    swapped = lax.all_to_all(scaled, "gx", split_axis=2, concat_axis=1, tiled=True)
    partial_gram = lax.dot_general(swapped, swapped, contract, precision=lax.Precision.HIGHEST)
    gram = lax.psum(partial_gram, ("gx", "gy", "gz"))
    basis = start_basis
    for step in range(ITERS):
        basis = orthonormal(jnp.dot(gram, basis, precision=lax.Precision.HIGHEST))
    along_rows = (((0,), (1,)), ((), ()))
    own_basis = lax.dynamic_slice_in_dim(basis, lax.axis_index("gx") * rows_dev, rows_dev, 0)
    core = lax.psum_scatter(
        lax.dot_general(own_basis, scaled, along_rows, precision=lax.Precision.HIGHEST),
        "gx",
        scatter_dimension=0,
        tiled=True,
    )
    return (basis, core)


def solution(mesh):
    in_specs = (P(None, "gx", "gy", "gz"), P(), P())
    out_specs = (P(), P("gx", None, "gy", "gz"))
    return jax.shard_map(
        per_device, mesh=mesh, in_specs=in_specs, out_specs=out_specs, check_vma=False
    )
```

profile of v0, /device:TPU:0, one launch (start us, length us, event | category | flops | bytes accessed | tf_op | source)
XLA Modules:
  0.0 333.2 jit_solution(15597270235788873526)
XLA Ops:
  7.2 0.0 copy-start
  7.2 0.0 all-reduce.2.cloned.1.call-start
  7.2 3.1 broadcast_multiply_fusion
  10.3 0.0 copy-start.1
  10.3 1.1 copy.24
  11.4 1.3 copy-done.1
  12.7 69.0 %all_to_all.18 = f32[11,125,8,128]{3,1,0,2:T(8,128)S(1)} all-to-all(f32[11,125,8,128]{3,1,0,2:T(8,128)S(1)} %copy.24), channel_id=1, replica_groups=mesh['gx'=4,'gy'=4,'gz'=2] {'gx'}, dimensions={2} | all-to-all | bytes 11264000 | tf_op jit(solution)/shard_map/all_to_all | solution.py:19
  81.7 2.9 copy.36
  84.6 6.2 %all_to_all.16 = f32[11,500,2,128]{3,1,2,0:T(8,128)} reshape(f32[11,4,125,2,128]{4,2,1,3,0:T(8,128)} %bitcast.67) | data formatting | bytes 11264000 | tf_op jit(solution)/shard_map/all_to_all | solution.py:19
  90.8 13.6 %convolution_bitcast_fusion = f32[500,500]{1,0:T(8,128)} fusion(f32[11,500,2,128]{3,1,2,0:T(8,128)} %all_to_all.16), kind=kOutput, calls=%fused_computation.4 | convolution fusion | flops 8448000000 | bytes 6632000 | tf_op jit(solution)/shard_map/dot_general | solution.py:20
  104.4 0.0 all-reduce.2.cloned.1.call-update
  104.4 0.2 reduce-scatter.2.cloned.1.call-start
  104.7 130.7 %all-reduce.2.cloned.1.call-done = f32[500,500]{1,0:T(8,128)} async-done(((f32[500,500]{1,0:T(8,128)}), f32[500,500]{1,0:T(8,128)}) %all-reduce.2.cloned.1.call-update) | async-done | bytes 1000016 | tf_op jit(solution)/shard_map/psum | solution.py:21
  235.4 0.0 copy-done
  235.4 2.3 fusion.24
  237.7 0.3 fusion.25
  238.0 0.1 copy.26
  238.0 5.8 %cholesky.59 = f32[64,64]{1,0:T(8,128)S(1)} custom-call(f32[64,64]{1,0:T(8,128)S(1)} %fusion.17), custom_call_target="Cholesky" | custom-call | tf_op jit(solution)/shard_map/jit(cholesky)/cholesky | solution.py:11
  243.9 0.6 compare_reduce_fusion.2
  244.6 0.7 fusion.8
  245.2 4.9 %custom-call.7 = f32[1,64,64]{1,2,0:T(8,128)S(1)} custom-call(f32[1,64,64]{2,1,0:T(8,128)S(1)} %fusion.8), custom_call_target="InvertDiagBlocksLowerTriangular" | custom-call | tf_op jit(solution)/shard_map/jit(_solve_triangular)/triangular_solve | solution.py:12
  250.1 0.3 fusion.6
  250.5 2.3 fusion.26
  252.8 0.3 fusion.27
  253.0 0.1 copy.27
  253.1 5.8 %cholesky.70 = f32[64,64]{1,0:T(8,128)S(1)} custom-call(f32[64,64]{1,0:T(8,128)S(1)} %fusion.15), custom_call_target="Cholesky" | custom-call | tf_op jit(solution)/shard_map/jit(cholesky)/cholesky | solution.py:11
  259.0 0.6 compare_reduce_fusion.1
  259.6 0.7 fusion.9
  260.3 4.9 %custom-call.8 = f32[1,64,64]{1,2,0:T(8,128)S(1)} custom-call(f32[1,64,64]{2,1,0:T(8,128)S(1)} %fusion.9), custom_call_target="InvertDiagBlocksLowerTriangular" | custom-call | tf_op jit(solution)/shard_map/jit(_solve_triangular)/triangular_solve | solution.py:12
  265.2 0.3 fusion.4
  265.5 2.3 fusion.28
  267.8 0.3 fusion.29
  268.1 0.1 copy.28
  268.2 5.8 %cholesky.81 = f32[64,64]{1,0:T(8,128)S(1)} custom-call(f32[64,64]{1,0:T(8,128)S(1)} %fusion.13), custom_call_target="Cholesky" | custom-call | tf_op jit(solution)/shard_map/jit(cholesky)/cholesky | solution.py:11
  274.1 0.6 compare_reduce_fusion
  274.7 0.7 fusion.10
  275.4 4.9 %custom-call.9 = f32[1,64,64]{1,2,0:T(8,128)S(1)} custom-call(f32[1,64,64]{2,1,0:T(8,128)S(1)} %fusion.10), custom_call_target="InvertDiagBlocksLowerTriangular" | custom-call | tf_op jit(solution)/shard_map/jit(_solve_triangular)/triangular_solve | solution.py:12
  280.3 0.3 fusion.2
  280.6 0.0 copy-start.2
  280.6 8.3 %fusion = f32[64,11,8,128]{3,0,2,1:T(8,128)} fusion(f32[11,125,8,128]{3,2,1,0:T(8,128)} %copy-done.1, f32[64,500]{1,0:T(8,128)S(1)} %fusion.2, s32[]{:T(128)S(6)} %select_n.6), kind=kOutput, calls=%fused_computation | convolution fusion | flops 1081344000 | bytes 8548356 | tf_op jit(solution)/shard_map/dot_general | solution.py:28
  288.9 0.0 reduce-scatter.2.cloned.1.call-update
  288.9 0.0 copy-done.2
  288.9 35.2 %reduce-scatter.2.cloned.1.call-done = f32[16,11,8,128]{3,0,2,1:T(8,128)} async-done(((f32[64,11,8,128]{3,0,2,1:T(8,128)}), f32[16,11,8,128]{3,0,2,1:T(8,128)}) %reduce-scatter.2.cloned.1.call-update) | async-done | bytes 720912 | tf_op jit(solution)/shard_map/reduce_scatter | solution.py:27
  324.2 2.2 copy.30
  (6 shorter events, 0.1 us)
Async XLA Ops:
  7.2 228.2 %copy-start = (f32[500,64]{0,1:T(8,128)S(1)}, f32[500,64]{0,1:T(8,128)}, u32[]{:S(2)}) copy-start(f32[500,64]{0,1:T(8,128)} %param.8) | copy-start | bytes 384004
  7.2 228.2 %all-reduce.2.cloned.1.call-start = ((), (), s32[]{:S(2)}) async-start(), calls=%async_computation.2 | async-start | bytes 2064384 | tf_op jit(solution)/shard_map/psum | solution.py:21
  10.3 2.4 copy-start.1
  104.4 219.7 %reduce-scatter.2.cloned.1.call-start = ((), (), s32[]{:S(2)}) async-start(), calls=%async_computation.3 | async-start | bytes 3604480 | tf_op jit(solution)/shard_map/reduce_scatter | solution.py:27
  280.6 8.3 %copy-start.2 = (f32[64,500]{1,0:T(8,128)}, f32[64,500]{1,0:T(8,128)S(1)}, u32[]{:S(2)}) copy-start(f32[64,500]{1,0:T(8,128)S(1)} %fusion.2) | copy-start | bytes 384004
Sparse Core Ops, SparseCore 0:
  104.6 130.7 all-reduce.1
  289.0 35.0 reduce-scatter.1
where the time goes:
time: 334 us; the launch traced here: 333 us
  waiting for transfers between devices  166 us (50%)
  blocking collectives  69 us (21%)
  other arithmetic  39.3 us (12%)
  matrix products  30.5 us (9%)
  between operations  14.2 us (4%)
  local copies, waits for them, and re-layouts  13.9 us (4%)
    psum x1, waiting for transfers between devices, per_device(): gram = lax.psum(partial_gram, ('gx', 'gy', 'gz'))  131 us
    all_to_all x1, blocking collectives, per_device(): lax.all_to_all(scaled, 'gx', split_axis=2, concat_axis=1, tiled=True)  69 us
    reduce_scatter x1, waiting for transfers between devices, per_device(): lax.psum_scatter(lax.dot_general(own_basis, scaled, along_rows, precision...  35.2 us
    another operation x9, other arithmetic, orthonormal(): lower = jnp.linalg.cholesky(small)  19.6 us
    another operation x6, other arithmetic, orthonormal(): return jax.scipy.linalg.solve_triangular(lower, block.T, lower=True).T  16.6 us
    dot_general x1, matrix products, per_device(): lax.dot_general(swapped, swapped, contract, precision=lax.Precision.HIGHEST)  13.6 us
    all_to_all x2, local copies, waits for them, and re-layouts, per_device(): lax.all_to_all(scaled, 'gx', split_axis=2, concat_axis=1, tiled=True)  9.05 us
    dot_general x1, matrix products, per_device(): lax.dot_general(own_basis, scaled, along_rows, precision=lax.Precision.HI...  8.26 us
  transfers between devices with their start and end apart: 2, of which 2 were waited for; matrix products, arithmetic and copies ran while one was open for 0% of the time, Pallas kernels for 0%

commit v1 on v0

--- a/solution.py
+++ b/solution.py
@@ -18,7 +18,7 @@
     contract = (((0, 2, 3), (0, 2, 3)), ((), ()))
     swapped = lax.all_to_all(scaled, "gx", split_axis=2, concat_axis=1, tiled=True)
     partial_gram = lax.dot_general(swapped, swapped, contract, precision=lax.Precision.HIGHEST)
-    gram = lax.psum(partial_gram, ("gx", "gy", "gz"))
+    gram = jnp.sum(lax.all_gather(partial_gram, ("gx", "gy", "gz")), axis=0)
     basis = start_basis
     for step in range(ITERS):
         basis = orthonormal(jnp.dot(gram, basis, precision=lax.Precision.HIGHEST))

time: 334 us -> 403 us (1.21)
  waiting for transfers between devices: 166 us -> 227 us
  other arithmetic: 39.3 us -> 51.4 us
    all_gather x0 -> x1, waiting for transfers between devices: none -> 192 us  [per_device(): gram = jnp.sum(lax.all_gather(partial_gram, ('gx', 'gy', 'gz')), axis=0)]
    psum x1 -> x0, waiting for transfers between devices: 131 us -> none  [per_device(): gram = lax.psum(partial_gram, ('gx', 'gy', 'gz'))]
    reduce_sum x0 -> x1, other arithmetic: none -> 12.2 us  [per_device(): gram = jnp.sum(lax.all_gather(partial_gram, ('gx', 'gy', 'gz')), axis=0)]
where the time goes in v1:
time: 403 us; the launch traced here: 402 us
  waiting for transfers between devices  227 us (56%)
  blocking collectives  69 us (17%)
  other arithmetic  51.4 us (13%)
  matrix products  26.8 us (7%)
  between operations  14.2 us (4%)
  local copies, waits for them, and re-layouts  14 us (3%)
    all_gather x1, waiting for transfers between devices, per_device(): gram = jnp.sum(lax.all_gather(partial_gram, ('gx', 'gy', 'gz')), axis=0)  192 us
    all_to_all x1, blocking collectives, per_device(): lax.all_to_all(scaled, 'gx', split_axis=2, concat_axis=1, tiled=True)  69 us
    reduce_scatter x1, waiting for transfers between devices, per_device(): lax.psum_scatter(lax.dot_general(own_basis, scaled, along_rows, precision...  34.4 us
    another operation x9, other arithmetic, orthonormal(): lower = jnp.linalg.cholesky(small)  19.6 us
    another operation x6, other arithmetic, orthonormal(): return jax.scipy.linalg.solve_triangular(lower, block.T, lower=True).T  16.6 us
    dot_general x1, matrix products, per_device(): lax.dot_general(swapped, swapped, contract, precision=lax.Precision.HIGHEST)  13.6 us
    reduce_sum x1, other arithmetic, per_device(): gram = jnp.sum(lax.all_gather(partial_gram, ('gx', 'gy', 'gz')), axis=0)  12.2 us
    all_to_all x2, local copies, waits for them, and re-layouts, per_device(): lax.all_to_all(scaled, 'gx', split_axis=2, concat_axis=1, tiled=True)  9.05 us
  transfers between devices with their start and end apart: 2, of which 2 were waited for; matrix products, arithmetic and copies ran while one was open for 0% of the time, Pallas kernels for 0%

profile of v1, /device:TPU:0, one launch (start us, length us, event | category | flops | bytes accessed | tf_op | source)
XLA Modules:
  0.0 402.2 jit_solution(17418091931119433425)
XLA Ops:
  7.2 0.0 copy-start
  7.2 0.0 all-gather.4.cloned.1.call-start
  7.2 3.1 broadcast_multiply_fusion
  10.3 0.0 copy-start.1
  10.3 1.1 copy.24
  11.4 1.4 copy-done.1
  12.8 69.0 %all_to_all.18 = f32[11,125,8,128]{3,1,0,2:T(8,128)S(1)} all-to-all(f32[11,125,8,128]{3,1,0,2:T(8,128)S(1)} %copy.24), channel_id=1, replica_groups=mesh['gx'=4,'gy'=4,'gz'=2] {'gx'}, dimensions={2} | all-to-all | bytes 11264000 | tf_op jit(solution)/shard_map/all_to_all | solution.py:19
  81.8 2.9 copy.36
  84.7 6.2 %all_to_all.16 = f32[11,500,2,128]{3,1,2,0:T(8,128)} reshape(f32[11,4,125,2,128]{4,2,1,3,0:T(8,128)} %bitcast.69) | data formatting | bytes 11264000 | tf_op jit(solution)/shard_map/all_to_all | solution.py:19
  90.9 13.6 %convolution_bitcast_fusion = f32[1,500,500]{2,1,0:T(8,128)} fusion(f32[11,500,2,128]{3,1,2,0:T(8,128)} %all_to_all.16), kind=kOutput, calls=%fused_computation.4 | convolution fusion | flops 8448000000 | bytes 6632000 | tf_op jit(solution)/shard_map/dot_general | solution.py:20
  104.5 0.0 all-gather.4.cloned.1.call-update
  104.5 0.0 reduce-scatter.2.cloned.1.call-start
  104.6 192.2 %all-gather.4.cloned.1.call-done = f32[32,500,500]{2,1,0:T(8,128)} async-done(((f32[1,500,500]{2,1,0:T(8,128)}), f32[32,500,500]{2,1,0:T(8,128)}) %all-gather.4.cloned.1.call-update) | async-done | bytes 32000016 | tf_op jit(solution)/shard_map/all_gather | solution.py:21
  296.7 12.2 %reduce_sum.9 = f32[500,500]{1,0:T(8,128)S(1)} reduce(f32[32,500,500]{2,1,0:T(8,128)} %all-gather.4.cloned.1.call-done, f32[]{:T(128)} %constant.39.clone.1), dimensions={0}, to_apply=%region_0.0 | reduce | flops 7750000 | bytes 33000004 | tf_op jit(solution)/shard_map/reduce_sum | solution.py:21
  308.9 0.0 copy-done
  308.9 1.1 fusion.24
  310.0 0.3 fusion.25
  310.2 0.1 copy.26
  310.3 5.8 %cholesky.59 = f32[64,64]{1,0:T(8,128)S(1)} custom-call(f32[64,64]{1,0:T(8,128)S(1)} %fusion.17), custom_call_target="Cholesky" | custom-call | tf_op jit(solution)/shard_map/jit(cholesky)/cholesky | solution.py:11
  316.2 0.6 compare_reduce_fusion.2
  316.9 0.7 fusion.8
  317.5 4.9 %custom-call.7 = f32[1,64,64]{1,2,0:T(8,128)S(1)} custom-call(f32[1,64,64]{2,1,0:T(8,128)S(1)} %fusion.8), custom_call_target="InvertDiagBlocksLowerTriangular" | custom-call | tf_op jit(solution)/shard_map/jit(_solve_triangular)/triangular_solve | solution.py:12
  322.4 0.3 fusion.6
  322.8 1.1 fusion.26
  323.8 0.3 fusion.27
  324.1 0.1 copy.27
  324.2 5.8 %cholesky.70 = f32[64,64]{1,0:T(8,128)S(1)} custom-call(f32[64,64]{1,0:T(8,128)S(1)} %fusion.15), custom_call_target="Cholesky" | custom-call | tf_op jit(solution)/shard_map/jit(cholesky)/cholesky | solution.py:11
  330.1 0.6 compare_reduce_fusion.1
  330.7 0.7 fusion.9
  331.4 4.9 %custom-call.8 = f32[1,64,64]{1,2,0:T(8,128)S(1)} custom-call(f32[1,64,64]{2,1,0:T(8,128)S(1)} %fusion.9), custom_call_target="InvertDiagBlocksLowerTriangular" | custom-call | tf_op jit(solution)/shard_map/jit(_solve_triangular)/triangular_solve | solution.py:12
  336.3 0.3 fusion.4
  336.6 1.1 fusion.28
  337.7 0.3 fusion.29
  337.9 0.1 copy.28
  338.0 5.8 %cholesky.81 = f32[64,64]{1,0:T(8,128)S(1)} custom-call(f32[64,64]{1,0:T(8,128)S(1)} %fusion.13), custom_call_target="Cholesky" | custom-call | tf_op jit(solution)/shard_map/jit(cholesky)/cholesky | solution.py:11
  343.9 0.6 compare_reduce_fusion
  344.6 0.7 fusion.10
  345.2 4.9 %custom-call.9 = f32[1,64,64]{1,2,0:T(8,128)S(1)} custom-call(f32[1,64,64]{2,1,0:T(8,128)S(1)} %fusion.10), custom_call_target="InvertDiagBlocksLowerTriangular" | custom-call | tf_op jit(solution)/shard_map/jit(_solve_triangular)/triangular_solve | solution.py:12
  350.1 0.3 fusion.2
  350.5 0.0 copy-start.2
  350.5 8.3 %fusion = f32[64,11,8,128]{3,0,2,1:T(8,128)} fusion(f32[11,125,8,128]{3,2,1,0:T(8,128)} %copy-done.1, f32[64,500]{1,0:T(8,128)S(1)} %fusion.2, s32[]{:T(128)S(6)} %select_n.6), kind=kOutput, calls=%fused_computation | convolution fusion | flops 1081344000 | bytes 8548356 | tf_op jit(solution)/shard_map/dot_general | solution.py:28
  358.8 0.0 reduce-scatter.2.cloned.1.call-update
  358.8 0.0 copy-done.2
  358.8 34.4 %reduce-scatter.2.cloned.1.call-done = f32[16,11,8,128]{3,0,2,1:T(8,128)} async-done(((f32[64,11,8,128]{3,0,2,1:T(8,128)}), f32[16,11,8,128]{3,0,2,1:T(8,128)}) %reduce-scatter.2.cloned.1.call-update) | async-done | bytes 720912 | tf_op jit(solution)/shard_map/reduce_scatter | solution.py:27
  393.2 2.2 copy.30
  (6 shorter events, 0.1 us)
Async XLA Ops:
  7.2 301.7 %copy-start = (f32[500,64]{0,1:T(8,128)S(1)}, f32[500,64]{0,1:T(8,128)}, u32[]{:S(2)}) copy-start(f32[500,64]{0,1:T(8,128)} %param.8) | copy-start | bytes 384004
  7.2 289.6 %all-gather.4.cloned.1.call-start = ((), (), s32[]{:S(2)}) async-start(), calls=%async_computation.3 | async-start | bytes 34062336 | tf_op jit(solution)/shard_map/all_gather | solution.py:21
  10.3 2.5 copy-start.1
  104.5 288.7 %reduce-scatter.2.cloned.1.call-start = ((), (), s32[]{:S(2)}) async-start(), calls=%async_computation.2 | async-start | bytes 3604480 | tf_op jit(solution)/shard_map/reduce_scatter | solution.py:27
  350.5 8.3 %copy-start.2 = (f32[64,500]{1,0:T(8,128)}, f32[64,500]{1,0:T(8,128)S(1)}, u32[]{:S(2)}) copy-start(f32[64,500]{1,0:T(8,128)S(1)} %fusion.2) | copy-start | bytes 384004
Sparse Core Ops, SparseCore 0:
  104.6 192.0 all-gather.3
  358.9 34.2 reduce-scatter.1
